TPU v7x, 512 devices: a 8x2x16 block of a 8x8x16 slice. The times are simulated.
512 devices in a mesh: prompt: 2 (over y), seq: 16 (over z), blk: 8 (over x), cfg: 2 (over core).
Axes of the slice: x: 8, y: 2, z: 16, core: 2. Of those that a mesh axis runs over, the one named last changes fastest.
The devices are a block of a 8x8x16 slice.
Arguments:
- queries: bfloat16 [2, 12288, 4096], P('cfg', ('prompt', 'blk', 'seq')), parts along dimension 1, may hold values from -5 to 5
- key_states: bfloat16 [2, 12288, 4096], P('cfg', ('prompt', 'blk', 'seq')), parts along dimension 1, may hold values from -5 to 5
- value_states: bfloat16 [2, 12288, 4096], P('cfg', ('prompt', 'blk', 'seq')), parts along dimension 1, may hold values from -6 to 6
- noisy_latents: float32 [12288, 64], P(('prompt', 'blk', 'seq')), parts along dimension 0, may hold values from -6 to 6
- patch_order: int32 [12288], P(('prompt', 'blk', 'seq')), parts along dimension 0, may hold values from 0 to 6143, as said below
- head_weight: bfloat16 [4096, 64], replicated, may hold values from -0.75 to 0.75
- latent_std: float32 [16], replicated, may hold values from 0.1 to 1.9
- latent_mean: float32 [16], replicated, may hold values from -3 to 3
- conv_weight: bfloat16 [3, 3, 3, 16, 384], replicated, may hold values from -0.3125 to 0.3125
- conv_bias: float32 [384], replicated, may hold values from -2 to 2
Outputs:
- features: bfloat16 [16, 64, 48, 384], P(('prompt', 'cfg'), 'seq', 'blk'), parts along dimension 0
There are 2 independent parts, one for each index of `prompt`. A program takes and returns all parts, laid end to end along the dimension named above; an argument that names none is the same for every part. Nothing has to cross between parts.
Inputs may be any that keep to these rules, and one draw needn't show every extreme that they name: A permutation of 0 to 6143 that keeps every aligned block of 48 tokens within itself: patch_order[t] // 48 == t // 48.
All inputs are finite; a program needn't handle non-finite values.
Results may differ from a plain program's by a relative error of at most 0.012.
Values may be sent and summed in bfloat16 or wider, within the bound.
A program may use at most 128 MiB of HBM per device.

v0:
```python
import math
import jax
import jax.numpy as jnp
from jax import lax
from jax.sharding import PartitionSpec as P

HDIM = 128
ZCH = 16
COLS_DEV = 3
GUIDE = 5.0
NOISE_LEVEL = 0.5


def split_up(array, dim, devices):
    lengths = array.shape
    pieces = array.reshape(*lengths[:dim], devices, lengths[dim] // devices, *lengths[dim + 1 :])
    return jnp.moveaxis(pieces, dim, 0)


def sum_at_owner(array, axis, dim):
    devices = lax.axis_size(axis)
    pieces = lax.all_to_all(split_up(array, dim, devices), axis, 0, 0, tiled=True)
    return jnp.sum(pieces.astype(jnp.float32), axis=0)


def partner(array, axis, apart):
    return lax.ppermute(array, axis, [(i, i ^ 1 << apart) for i in range(lax.axis_size(axis))])


def padded(array, sides, width):
    for axis, dim in sides:
        devices, length = (lax.axis_size(axis), array.shape[dim])
        up = [(i, (i + 1) % devices) for i in range(devices - 1)]
        down = [(j, i) for i, j in up]
        last = lax.slice_in_dim(array, length - width, length, axis=dim)
        first = lax.slice_in_dim(array, 0, width, axis=dim)
        before = lax.ppermute(last, axis, up)
        after = lax.ppermute(first, axis, down)
        array = jnp.concatenate([before, array, after], axis=dim)
    return array


def fold_keys(carry, piece, grouped, block):
    keys_piece, values_piece = piece
    heads = grouped.shape[1]
    count = keys_piece.shape[0] // block
    key_blocks = keys_piece.reshape(count, block, heads, HDIM)
    value_blocks = values_piece.reshape(count, block, heads, HDIM)
    scale = 1.0 / math.sqrt(HDIM)

    def one_block(state, pair):
        top, total, acc = state
        key_block, value_block = pair
        scores = (
            jnp.einsum("qhd,khd->hqk", grouped, key_block, preferred_element_type=jnp.float32)
            * scale
        )
        new_top = jnp.maximum(top, jnp.max(scores, axis=2))
        expo = jnp.exp(scores - new_top[:, :, None])
        factor = jnp.exp(top - new_top)
        total = total * factor + jnp.sum(expo, axis=2)
        weights = expo.astype(jnp.bfloat16)
        update = jnp.einsum(
            "hqk,khd->qhd", weights, value_block, preferred_element_type=jnp.float32
        )
        acc = acc * factor.T[:, :, None] + update
        return ((new_top, total, acc), None)

    state, unused = lax.scan(one_block, carry, (key_blocks, value_blocks))
    return state


def start_for(rows, heads):
    return (
        jnp.full((heads, rows), -1e30, jnp.float32),
        jnp.zeros((heads, rows), jnp.float32),
        jnp.zeros((rows, heads, HDIM), jnp.float32),
    )


def finish(state):
    top, total, acc = state
    rows = acc.shape[0]
    return (acc / total.T[:, :, None]).astype(jnp.bfloat16).reshape(rows, acc.shape[1] * HDIM)


def local(
    queries,
    key_states,
    value_states,
    noisy_latents,
    patch_order,
    head_weight,
    latent_std,
    latent_mean,
    conv_weight,
    conv_bias,
):
    seq_count = lax.axis_size("seq")
    blk_count = lax.axis_size("blk")
    seq_index = lax.axis_index("seq")
    blk_index = lax.axis_index("blk")
    cfg_index = lax.axis_index("cfg")
    tok_rows = queries.shape[1]
    own_query = queries[0]
    own_keys = key_states[0]
    own_values = value_states[0]
    local_query, local_keys, local_values = (
        lax.all_to_all(own_query, "seq", split_axis=1, concat_axis=0, tiled=True),
        lax.all_to_all(own_keys, "seq", split_axis=1, concat_axis=0, tiled=True),
        lax.all_to_all(own_values, "seq", split_axis=1, concat_axis=0, tiled=True),
    )
    frame_rows = local_query.shape[0]
    heads = local_query.shape[1] // HDIM
    grouped = local_query.reshape(frame_rows, heads, HDIM)
    state = fold_keys(
        start_for(frame_rows, heads),
        (
            lax.all_gather(local_keys, "blk", axis=0, tiled=True),
            lax.all_gather(local_values, "blk", axis=0, tiled=True),
        ),
        grouped,
        frame_rows,
    )
    attended = finish(state)
    weight_rows = lax.dynamic_slice_in_dim(
        head_weight, seq_index * attended.shape[1], attended.shape[1], 0
    )
    velocity = sum_at_owner(
        jnp.dot(attended, weight_rows, preferred_element_type=jnp.float32).astype(jnp.bfloat16),
        "seq",
        0,
    )
    other = partner(velocity, "cfg", 0)
    is_cond = cfg_index == 0
    cond = jnp.where(is_cond, velocity, other)
    uncond = jnp.where(is_cond, other, velocity)
    guided = uncond + GUIDE * (cond - uncond)
    denoised = noisy_latents - NOISE_LEVEL * guided
    pixels = (
        denoised * jnp.tile(latent_std, 4)[None, :] + jnp.tile(latent_mean, 4)[None, :]
    ).astype(jnp.bfloat16)
    block_start = (blk_index * seq_count + seq_index) * tok_rows
    local_slot = patch_order - block_start
    selector = (jnp.arange(tok_rows, dtype=jnp.int32)[:, None] == local_slot[None, :]).astype(
        jnp.bfloat16
    )
    placed = jnp.dot(selector, pixels, preferred_element_type=jnp.float32).astype(jnp.bfloat16)
    grid_cols = COLS_DEV * blk_count
    strip_rows = tok_rows // grid_cols
    strip = placed.reshape(1, strip_rows, grid_cols * placed.shape[1])
    received = lax.all_to_all(strip, "blk", split_axis=2, concat_axis=0, tiled=True)
    frame_count = received.shape[0]
    tile = (
        received.reshape(frame_count, strip_rows, COLS_DEV, 2, 2, ZCH)
        .transpose(0, 1, 3, 2, 4, 5)
        .reshape(frame_count, 2 * strip_rows, 2 * COLS_DEV, ZCH)
    )
    half = frame_count // 2
    leading = jnp.zeros((2,) + tile.shape[1:], jnp.bfloat16)
    timeline = jnp.concatenate([leading, tile], axis=0)
    window = lax.dynamic_slice_in_dim(timeline, cfg_index * half, half + 2, 0)
    framed = padded(window, (("seq", 1), ("blk", 2)), 1)
    tile_rows = 2 * strip_rows
    tile_cols = 2 * COLS_DEV
    columns = []
    for step_t in range(3):
        for step_y in range(3):
            for step_x in range(3):
                columns.append(
                    framed[
                        step_t : step_t + half,
                        step_y : step_y + tile_rows,
                        step_x : step_x + tile_cols,
                        :,
                    ]
                )
    stacked = jnp.concatenate(columns, axis=3).reshape(half * tile_rows * tile_cols, 27 * ZCH)
    kernel = conv_weight.reshape(27 * ZCH, conv_weight.shape[4])
    output = jnp.dot(stacked, kernel, preferred_element_type=jnp.float32) + conv_bias[None, :]
    return output.reshape(half, tile_rows, tile_cols, conv_weight.shape[4]).astype(jnp.bfloat16)


def solution(mesh):
    in_specs = (
        P("cfg", ("prompt", "blk", "seq"), None),
        P("cfg", ("prompt", "blk", "seq"), None),
        P("cfg", ("prompt", "blk", "seq"), None),
        P(("prompt", "blk", "seq"), None),
        P(("prompt", "blk", "seq")),
        P(),
        P(),
        P(),
        P(),
        P(),
    )
    out_specs = P(("prompt", "cfg"), "seq", "blk", None)
    return jax.shard_map(local, mesh=mesh, in_specs=in_specs, out_specs=out_specs, check_vma=False)
```

profile of v0, /device:TPU:66, one launch (start us, length us, event | category | flops | bytes accessed | tf_op | source)
XLA Modules:
  0.0 339.0 jit_solution(12205130973058300356)
XLA Ops:
  6.6 1.2 copy.77
  7.8 67.3 %all_to_all.74 = bf16[48,16,256]{2,0,1:T(8,128)(2,1)} all-to-all(bf16[48,16,256]{2,0,1:T(8,128)(2,1)S(1)} %copy.52), channel_id=1, replica_groups=mesh['prompt'=2,'seq'=16,'blk'=8,'cfg'=2] {'seq'}, dimensions={1} | all-to-all | bytes 786432 | tf_op jit(solution)/shard_map/all_to_all | solution.py:110
  75.3 1.1 copy.79
  76.5 29.7 %all_to_all.75 = bf16[48,16,256]{2,0,1:T(8,128)(2,1)} all-to-all(bf16[48,16,256]{2,0,1:T(8,128)(2,1)S(1)} %copy.55), channel_id=1, replica_groups=mesh['prompt'=2,'seq'=16,'blk'=8,'cfg'=2] {'seq'}, dimensions={1} | all-to-all | bytes 786432 | tf_op jit(solution)/shard_map/all_to_all | solution.py:111
  106.3 0.9 copy.54
  107.2 6.2 %all-to-all-start.1 = ((bf16[48,16,256]{2,0,1:T(8,128)(2,1)}), bf16[48,16,256]{2,0,1:T(8,128)(2,1)S(1)}, u32[]{:S(2)}, u32[]{:S(2)}) async-start(bf16[48,16,256]{2,0,1:T(8,128)(2,1)} %copy.54), calls=%async_computation.1 | async-start | bytes 786432 | tf_op jit(solution)/shard_map/all_to_all | solution.py:109
  113.4 23.1 %all-to-all-done.1 = bf16[48,16,256]{2,0,1:T(8,128)(2,1)S(1)} async-done(((bf16[48,16,256]{2,0,1:T(8,128)(2,1)}), bf16[48,16,256]{2,0,1:T(8,128)(2,1)S(1)}, u32[]{:S(2)}, u32[]{:S(2)}) %all-to-all-start.1) | async-done | bytes 393248 | tf_op jit(solution)/shard_map/all_to_all | solution.py:109
  136.7 5.5 %reshape.65 = bf16[8,768,2,128]{3,2,1,0:T(2,128)(2,1)} reshape(bf16[6144,256]{1,0:T(8,128)(2,1)} %all-gather.3.cloned.1.call-done) | data formatting | bytes 6291456 | tf_op jit(solution)/shard_map/reshape | solution.py:47
  142.2 32.6 %all-gather.5.cloned.1.call-done = bf16[6144,256]{1,0:T(8,128)(2,1)} async-done(((bf16[768,256]{1,0:T(8,128)(2,1)}), bf16[6144,256]{1,0:T(8,128)(2,1)}) %all-gather.5.cloned.1.call-update) | async-done | bytes 3145744 | tf_op jit(solution)/shard_map/all_gather | solution.py:120
  174.8 5.5 %reshape.66 = bf16[8,768,2,128]{3,2,1,0:T(2,128)(2,1)} reshape(bf16[6144,256]{1,0:T(8,128)(2,1)} %all-gather.5.cloned.1.call-done) | data formatting | bytes 6291456 | tf_op jit(solution)/shard_map/reshape | solution.py:48
  180.3 77.1 %while.15 = (s32[]{:T(128)}, f32[2,768]{1,0:T(2,128)S(1)}, f32[2,768]{1,0:T(2,128)S(1)}, f32[768,2,128]{0,2,1:T(8,128)S(1)}, bf16[8,768,2,128]{3,2,1,0:T(2,128)(...) while((s32[]{:T(128)}, f32[2,768]{1,0:T(2,128)S(1)}, ...), condition=%wide.region_3.4_spmd.clone, body=%wide.region_0.3_spmd.clone.sunk | while | flops 614016000 | bytes 38240392 | solution.py:69
  180.3 1.7 constant_dynamic-slice_fusion.3
  182.0 2.9 bitcast_reduce_fusion.2
  185.4 3.6 %fusion.54 = f32[768,2,128]{0,2,1:T(8,128)S(1)} fusion(f32[2,768,768]{2,1,0:T(8,128)} %get-tuple-element.214, f32[2,768]{1,0:T(2,128)S(1)} %get-tuple-element.236, f32[768,2,128]{0,2,1:T(8,128)S(1)} %get-tuple-element.229, bf16[1,768,2,128]{1,3,2,0:T(8,128)(2,1)S(1)} %copy.87, f32[768,2]{0,1:T(2,128)S(1)} %get-tuple-element.216, pred[]{:T(512)S(6)} %compare.4), kind=kOutput, calls=%fused_computation.9.clone.1 | convolution fusion | flops 306118656 | bytes 6696961 | tf_op jit(solution)/shard_map/while/body/eval_jaxpr/hqk,khd->qhd/dot_general | solution.py:63
  189.1 0.8 fusion.52
  190.0 1.7 constant_dynamic-slice_fusion.3
  191.6 2.9 bitcast_reduce_fusion.2
  195.0 3.6 %fusion.54 = f32[768,2,128]{0,2,1:T(8,128)S(1)} fusion(f32[2,768,768]{2,1,0:T(8,128)} %get-tuple-element.214, f32[2,768]{1,0:T(2,128)S(1)} %get-tuple-element.236, f32[768,2,128]{0,2,1:T(8,128)S(1)} %get-tuple-element.229, bf16[1,768,2,128]{1,3,2,0:T(8,128)(2,1)S(1)} %copy.87, f32[768,2]{0,1:T(2,128)S(1)} %get-tuple-element.216, pred[]{:T(512)S(6)} %compare.4), kind=kOutput, calls=%fused_computation.9.clone.1 | convolution fusion | flops 306118656 | bytes 6696961 | tf_op jit(solution)/shard_map/while/body/eval_jaxpr/hqk,khd->qhd/dot_general | solution.py:63
  198.8 0.8 fusion.52
  199.6 1.7 constant_dynamic-slice_fusion.3
  201.3 2.9 bitcast_reduce_fusion.2
  204.6 3.6 %fusion.54 = f32[768,2,128]{0,2,1:T(8,128)S(1)} fusion(f32[2,768,768]{2,1,0:T(8,128)} %get-tuple-element.214, f32[2,768]{1,0:T(2,128)S(1)} %get-tuple-element.236, f32[768,2,128]{0,2,1:T(8,128)S(1)} %get-tuple-element.229, bf16[1,768,2,128]{1,3,2,0:T(8,128)(2,1)S(1)} %copy.87, f32[768,2]{0,1:T(2,128)S(1)} %get-tuple-element.216, pred[]{:T(512)S(6)} %compare.4), kind=kOutput, calls=%fused_computation.9.clone.1 | convolution fusion | flops 306118656 | bytes 6696961 | tf_op jit(solution)/shard_map/while/body/eval_jaxpr/hqk,khd->qhd/dot_general | solution.py:63
  208.4 0.8 fusion.52
  209.2 1.7 constant_dynamic-slice_fusion.3
  210.9 2.9 bitcast_reduce_fusion.2
  214.3 3.6 %fusion.54 = f32[768,2,128]{0,2,1:T(8,128)S(1)} fusion(f32[2,768,768]{2,1,0:T(8,128)} %get-tuple-element.214, f32[2,768]{1,0:T(2,128)S(1)} %get-tuple-element.236, f32[768,2,128]{0,2,1:T(8,128)S(1)} %get-tuple-element.229, bf16[1,768,2,128]{1,3,2,0:T(8,128)(2,1)S(1)} %copy.87, f32[768,2]{0,1:T(2,128)S(1)} %get-tuple-element.216, pred[]{:T(512)S(6)} %compare.4), kind=kOutput, calls=%fused_computation.9.clone.1 | convolution fusion | flops 306118656 | bytes 6696961 | tf_op jit(solution)/shard_map/while/body/eval_jaxpr/hqk,khd->qhd/dot_general | solution.py:63
  218.0 0.8 fusion.52
  218.9 1.7 constant_dynamic-slice_fusion.3
  220.5 2.9 bitcast_reduce_fusion.2
  223.9 3.6 %fusion.54 = f32[768,2,128]{0,2,1:T(8,128)S(1)} fusion(f32[2,768,768]{2,1,0:T(8,128)} %get-tuple-element.214, f32[2,768]{1,0:T(2,128)S(1)} %get-tuple-element.236, f32[768,2,128]{0,2,1:T(8,128)S(1)} %get-tuple-element.229, bf16[1,768,2,128]{1,3,2,0:T(8,128)(2,1)S(1)} %copy.87, f32[768,2]{0,1:T(2,128)S(1)} %get-tuple-element.216, pred[]{:T(512)S(6)} %compare.4), kind=kOutput, calls=%fused_computation.9.clone.1 | convolution fusion | flops 306118656 | bytes 6696961 | tf_op jit(solution)/shard_map/while/body/eval_jaxpr/hqk,khd->qhd/dot_general | solution.py:63
  227.7 0.8 fusion.52
  228.5 1.7 constant_dynamic-slice_fusion.3
  230.2 2.9 bitcast_reduce_fusion.2
  233.6 3.6 %fusion.54 = f32[768,2,128]{0,2,1:T(8,128)S(1)} fusion(f32[2,768,768]{2,1,0:T(8,128)} %get-tuple-element.214, f32[2,768]{1,0:T(2,128)S(1)} %get-tuple-element.236, f32[768,2,128]{0,2,1:T(8,128)S(1)} %get-tuple-element.229, bf16[1,768,2,128]{1,3,2,0:T(8,128)(2,1)S(1)} %copy.87, f32[768,2]{0,1:T(2,128)S(1)} %get-tuple-element.216, pred[]{:T(512)S(6)} %compare.4), kind=kOutput, calls=%fused_computation.9.clone.1 | convolution fusion | flops 306118656 | bytes 6696961 | tf_op jit(solution)/shard_map/while/body/eval_jaxpr/hqk,khd->qhd/dot_general | solution.py:63
  237.3 0.8 fusion.52
  238.1 1.7 constant_dynamic-slice_fusion.3
  239.8 2.9 bitcast_reduce_fusion.2
  243.2 3.6 %fusion.54 = f32[768,2,128]{0,2,1:T(8,128)S(1)} fusion(f32[2,768,768]{2,1,0:T(8,128)} %get-tuple-element.214, f32[2,768]{1,0:T(2,128)S(1)} %get-tuple-element.236, f32[768,2,128]{0,2,1:T(8,128)S(1)} %get-tuple-element.229, bf16[1,768,2,128]{1,3,2,0:T(8,128)(2,1)S(1)} %copy.87, f32[768,2]{0,1:T(2,128)S(1)} %get-tuple-element.216, pred[]{:T(512)S(6)} %compare.4), kind=kOutput, calls=%fused_computation.9.clone.1 | convolution fusion | flops 306118656 | bytes 6696961 | tf_op jit(solution)/shard_map/while/body/eval_jaxpr/hqk,khd->qhd/dot_general | solution.py:63
  246.9 0.8 fusion.52
  247.8 1.7 constant_dynamic-slice_fusion.3
  249.4 2.9 bitcast_reduce_fusion.2
  252.8 3.6 %fusion.54 = f32[768,2,128]{0,2,1:T(8,128)S(1)} fusion(f32[2,768,768]{2,1,0:T(8,128)} %get-tuple-element.214, f32[2,768]{1,0:T(2,128)S(1)} %get-tuple-element.236, f32[768,2,128]{0,2,1:T(8,128)S(1)} %get-tuple-element.229, bf16[1,768,2,128]{1,3,2,0:T(8,128)(2,1)S(1)} %copy.87, f32[768,2]{0,1:T(2,128)S(1)} %get-tuple-element.216, pred[]{:T(512)S(6)} %compare.4), kind=kOutput, calls=%fused_computation.9.clone.1 | convolution fusion | flops 306118656 | bytes 6696961 | tf_op jit(solution)/shard_map/while/body/eval_jaxpr/hqk,khd->qhd/dot_general | solution.py:63
  256.6 0.8 fusion.52
  257.9 0.8 reshape.67
  258.7 13.1 %all-to-all-start.3 = ((bf16[16,2,1536]{2,1,0:T(2,128)(2,1)}), bf16[16,2,1536]{2,1,0:T(2,128)(2,1)S(1)}, u32[]{:S(2)}, u32[]{:S(2)}) async-start(bf16[16,2,1536]{2,1,0:T(2,128)(2,1)} %reshape.67), calls=%async_computation.3 | async-start | bytes 196608 | tf_op jit(solution)/shard_map/all_to_all | solution.py:22
  271.8 12.9 %all-to-all-done.3 = bf16[16,2,1536]{2,1,0:T(2,128)(2,1)S(1)} async-done(((bf16[16,2,1536]{2,1,0:T(2,128)(2,1)}), bf16[16,2,1536]{2,1,0:T(2,128)(2,1)S(1)}, u32[]{:S(2)}, u32[]{:S(2)}) %all-to-all-start.3) | async-done | bytes 98336 | tf_op jit(solution)/shard_map/all_to_all | solution.py:22
  285.0 2.1 collective-permute-start
  287.5 0.7 collective-permute-done
  288.5 0.7 copy.63
  289.1 0.5 broadcast.58
  289.6 8.8 %reduce = bf16[1536,2]{1,0:T(8,128)(2,1)S(1)} reduce(bf16[1536,1,2]{2,1,0:T(2,128)(2,1)S(1)} %bitcast.77, bf16[]{:T(256)} %broadcast.58), dimensions={1}, to_apply=%bitcast.53.reduce_sub_computation | reduce | bytes 12290
  298.5 1.1 reshape.69
  299.6 5.7 %all-to-all-start.4 = ((bf16[8,2,192]{2,1,0:T(2,128)(2,1)}), bf16[8,2,192]{2,1,0:T(2,128)(2,1)S(1)}, u32[]{:S(2)}, u32[]{:S(2)}) async-start(bf16[8,2,192]{2,1,0:T(2,128)(2,1)} %reshape.69), calls=%async_computation.4 | async-start | bytes 16384 | tf_op jit(solution)/shard_map/all_to_all | solution.py:152
  305.3 6.3 %all-to-all-done.4 = bf16[8,2,192]{2,1,0:T(2,128)(2,1)S(1)} async-done(((bf16[8,2,192]{2,1,0:T(2,128)(2,1)}), bf16[8,2,192]{2,1,0:T(2,128)(2,1)S(1)}, u32[]{:S(2)}, u32[]{:S(2)}) %all-to-all-start.4) | async-done | bytes 6176 | tf_op jit(solution)/shard_map/all_to_all | solution.py:152
  311.6 0.9 reshape.70
  312.5 0.5 copy.64
  313.3 2.9 collective-permute-start.1
  316.2 1.3 collective-permute-start.2
  317.7 4.1 %collective-permute-done.2 = bf16[6,1,6,16]{3,0,2,1:T(8,128)(2,1)S(1)} collective-permute-done((bf16[6,1,6,16]{3,0,2,1:T(8,128)(2,1)S(1)}, bf16[6,1,6,16]{3,0,2,1:T(8,128)(2,1)S(1)}, u32[]{:S(2)}, u32[]{:S(2)}) %collective-permute-start.2) | collective-permute-done | bytes 1184 | tf_op jit(solution)/shard_map/ppermute | solution.py:38
  321.8 2.5 collective-permute-start.3
  324.3 3.4 %collective-permute-start.4 = (bf16[6,6,1,16]{3,0,2,1:T(8,128)(2,1)S(1)}, bf16[6,6,1,16]{3,0,2,1:T(8,128)(2,1)S(1)}, u32[]{:S(2)}, u32[]{:S(2)}) collective-permute-start(bf16[6,6,1,16]{3,0,2,1:T(8,128)(2,1)S(1)} %get-tuple-element.137), channel_id=1, source_target_pairs={{2,0},{4,2},{6,4},{8,6},{10,8},{12,10},{14,12},{3,1},{5,3},{7,5},{... | collective-permute-start | bytes 3464 | tf_op jit(solution)/shard_map/ppermute | solution.py:38
  327.8 2.1 collective-permute-done.4
  330.1 1.0 concatenate.48
  331.5 0.7 copy.67
  (107 shorter events, 7.6 us)
Async XLA Ops:
  6.5 251.0 %copy-start = (bf16[4096,64]{0,1:T(8,128)(2,1)S(1)}, bf16[4096,64]{0,1:T(8,128)(2,1)}, u32[]{:S(2)}) copy-start(bf16[4096,64]{0,1:T(8,128)(2,1)} %param.17) | copy-start | bytes 1572868
  6.6 99.6 %copy-start.2 = (bf16[1,48,4096]{2,1,0:T(8,128)(2,1)S(1)}, bf16[1,48,4096]{2,1,0:T(8,128)(2,1)}, u32[]{:S(2)}) copy-start(bf16[1,48,4096]{2,1,0:T(8,128)(2,1)} %param.12) | copy-start | bytes 1179652
  6.6 130.1 %all-gather.3.cloned.1.call-start = ((), (), s32[]{:S(2)}) async-start(), calls=%async_computation.5 | async-start | bytes 3538944 | tf_op jit(solution)/shard_map/all_gather | solution.py:119
  75.2 99.6 %all-gather.5.cloned.1.call-start = ((), (), s32[]{:S(2)}) async-start(), calls=%async_computation.6 | async-start | bytes 3538944 | tf_op jit(solution)/shard_map/all_gather | solution.py:120
  107.2 29.3 %all-to-all-start.1 = ((bf16[48,16,256]{2,0,1:T(8,128)(2,1)}), bf16[48,16,256]{2,0,1:T(8,128)(2,1)S(1)}, u32[]{:S(2)}, u32[]{:S(2)}) async-start(bf16[48,16,256]{2,0,1:T(8,128)(2,1)} %copy.54), calls=%async_computation.1 | async-start | bytes 786432 | tf_op jit(solution)/shard_map/all_to_all | solution.py:109
  180.3 106.9 %copy-start.8 = (s32[48]{0:T(128)S(1)}, s32[48]{0:T(128)}, u32[]{:S(2)}) copy-start(s32[48]{0:T(128)} %param.16) | copy-start | bytes 580
  180.3 106.9 %copy-start.4 = (f32[48,64]{1,0:T(8,128)S(1)}, f32[48,64]{1,0:T(8,128)}, u32[]{:S(2)}) copy-start(f32[48,64]{1,0:T(8,128)} %param.15) | copy-start | bytes 36868
  180.3 107.0 %copy-start.6 = (f32[16]{0:T(128)S(1)}, f32[16]{0:T(128)}, u32[]{:S(2)}) copy-start(f32[16]{0:T(128)} %param.19) | copy-start | bytes 196
  180.3 107.1 %copy-start.7 = (f32[16]{0:T(128)S(1)}, f32[16]{0:T(128)}, u32[]{:S(2)}) copy-start(f32[16]{0:T(128)} %param.18) | copy-start | bytes 196
  185.4 3.8 %copy-start.1 = (f32[2,768,768]{2,1,0:T(8,128)S(1)}, f32[2,768,768]{2,1,0:T(8,128)}, u32[]{:S(2)}) copy-start(f32[2,768,768]{2,1,0:T(8,128)} %get-tuple-element.214) | copy-start | bytes 14155780 | tf_op jit(solution)/shard_map/while
  195.0 3.8 %copy-start.1 = (f32[2,768,768]{2,1,0:T(8,128)S(1)}, f32[2,768,768]{2,1,0:T(8,128)}, u32[]{:S(2)}) copy-start(f32[2,768,768]{2,1,0:T(8,128)} %get-tuple-element.214) | copy-start | bytes 14155780 | tf_op jit(solution)/shard_map/while
  204.6 3.8 %copy-start.1 = (f32[2,768,768]{2,1,0:T(8,128)S(1)}, f32[2,768,768]{2,1,0:T(8,128)}, u32[]{:S(2)}) copy-start(f32[2,768,768]{2,1,0:T(8,128)} %get-tuple-element.214) | copy-start | bytes 14155780 | tf_op jit(solution)/shard_map/while
  214.3 3.8 %copy-start.1 = (f32[2,768,768]{2,1,0:T(8,128)S(1)}, f32[2,768,768]{2,1,0:T(8,128)}, u32[]{:S(2)}) copy-start(f32[2,768,768]{2,1,0:T(8,128)} %get-tuple-element.214) | copy-start | bytes 14155780 | tf_op jit(solution)/shard_map/while
  223.9 3.8 %copy-start.1 = (f32[2,768,768]{2,1,0:T(8,128)S(1)}, f32[2,768,768]{2,1,0:T(8,128)}, u32[]{:S(2)}) copy-start(f32[2,768,768]{2,1,0:T(8,128)} %get-tuple-element.214) | copy-start | bytes 14155780 | tf_op jit(solution)/shard_map/while
  233.5 3.8 %copy-start.1 = (f32[2,768,768]{2,1,0:T(8,128)S(1)}, f32[2,768,768]{2,1,0:T(8,128)}, u32[]{:S(2)}) copy-start(f32[2,768,768]{2,1,0:T(8,128)} %get-tuple-element.214) | copy-start | bytes 14155780 | tf_op jit(solution)/shard_map/while
  243.2 3.8 %copy-start.1 = (f32[2,768,768]{2,1,0:T(8,128)S(1)}, f32[2,768,768]{2,1,0:T(8,128)}, u32[]{:S(2)}) copy-start(f32[2,768,768]{2,1,0:T(8,128)} %get-tuple-element.214) | copy-start | bytes 14155780 | tf_op jit(solution)/shard_map/while
  252.8 3.8 %copy-start.1 = (f32[2,768,768]{2,1,0:T(8,128)S(1)}, f32[2,768,768]{2,1,0:T(8,128)}, u32[]{:S(2)}) copy-start(f32[2,768,768]{2,1,0:T(8,128)} %get-tuple-element.214) | copy-start | bytes 14155780 | tf_op jit(solution)/shard_map/while
  257.5 73.7 %copy-start.3 = (bf16[3,3,3,16,384]{4,3,2,1,0:T(8,128)(2,1)S(1)}, bf16[3,3,3,16,384]{4,3,2,1,0:T(8,128)(2,1)}, u32[]{:S(2)}) copy-start(bf16[3,3,3,16,384]{4,3,2,1,0:T(8,128)(2,1)} %param.20) | copy-start | bytes 995332
  257.5 73.7 %copy-start.5 = (f32[384]{0:T(512)S(1)}, f32[384]{0:T(512)}, u32[]{:S(2)}) copy-start(f32[384]{0:T(512)} %param.21) | copy-start | bytes 4612
  258.7 26.0 %all-to-all-start.3 = ((bf16[16,2,1536]{2,1,0:T(2,128)(2,1)}), bf16[16,2,1536]{2,1,0:T(2,128)(2,1)S(1)}, u32[]{:S(2)}, u32[]{:S(2)}) async-start(bf16[16,2,1536]{2,1,0:T(2,128)(2,1)} %reshape.67), calls=%async_computation.3 | async-start | bytes 196608 | tf_op jit(solution)/shard_map/all_to_all | solution.py:22
  285.0 3.1 collective-permute-start
  299.6 12.0 %all-to-all-start.4 = ((bf16[8,2,192]{2,1,0:T(2,128)(2,1)}), bf16[8,2,192]{2,1,0:T(2,128)(2,1)S(1)}, u32[]{:S(2)}, u32[]{:S(2)}) async-start(bf16[8,2,192]{2,1,0:T(2,128)(2,1)} %reshape.69), calls=%async_computation.4 | async-start | bytes 16384 | tf_op jit(solution)/shard_map/all_to_all | solution.py:152
  313.3 4.4 %collective-permute-start.1 = (bf16[6,1,6,16]{3,0,2,1:T(8,128)(2,1)S(1)}, bf16[6,1,6,16]{3,0,2,1:T(8,128)(2,1)S(1)}, u32[]{:S(2)}, u32[]{:S(2)}) collective-permute-start(bf16[6,1,6,16]{3,0,2,1:T(8,128)(2,1)S(1)} %get-tuple-element.151), channel_id=1, source_target_pairs={{0,16},{16,32},{32,48},{48,64},{64,80},{80,96},{96,112},{112,128},... | collective-permute-start | bytes 3464 | tf_op jit(solution)/shard_map/ppermute | solution.py:37
  316.2 5.6 %collective-permute-start.2 = (bf16[6,1,6,16]{3,0,2,1:T(8,128)(2,1)S(1)}, bf16[6,1,6,16]{3,0,2,1:T(8,128)(2,1)S(1)}, u32[]{:S(2)}, u32[]{:S(2)}) collective-permute-start(bf16[6,1,6,16]{3,0,2,1:T(8,128)(2,1)S(1)} %get-tuple-element.152), channel_id=1, source_target_pairs={{16,0},{32,16},{48,32},{64,48},{80,64},{96,80},{112,96},{128,112},... | collective-permute-start | bytes 3464 | tf_op jit(solution)/shard_map/ppermute | solution.py:38
  321.8 6.0 %collective-permute-start.3 = (bf16[6,6,1,16]{3,0,2,1:T(8,128)(2,1)S(1)}, bf16[6,6,1,16]{3,0,2,1:T(8,128)(2,1)S(1)}, u32[]{:S(2)}, u32[]{:S(2)}) collective-permute-start(bf16[6,6,1,16]{3,0,2,1:T(8,128)(2,1)S(1)} %get-tuple-element.138), channel_id=1, source_target_pairs={{0,2},{2,4},{4,6},{6,8},{8,10},{10,12},{12,14},{1,3},{3,5},{5,7},{... | collective-permute-start | bytes 3464 | tf_op jit(solution)/shard_map/ppermute | solution.py:37
  324.3 5.6 %collective-permute-start.4 = (bf16[6,6,1,16]{3,0,2,1:T(8,128)(2,1)S(1)}, bf16[6,6,1,16]{3,0,2,1:T(8,128)(2,1)S(1)}, u32[]{:S(2)}, u32[]{:S(2)}) collective-permute-start(bf16[6,6,1,16]{3,0,2,1:T(8,128)(2,1)S(1)} %get-tuple-element.137), channel_id=1, source_target_pairs={{2,0},{4,2},{6,4},{8,6},{10,8},{12,10},{14,12},{3,1},{5,3},{7,5},{... | collective-permute-start | bytes 3464 | tf_op jit(solution)/shard_map/ppermute | solution.py:38
Sparse Core Ops, SparseCore 0:
  75.3 46.9 all-gather.2
  124.4 50.3 all-gather.4
where the time goes:
time: 340 us; the launch traced here: 339 us
  blocking collectives  97 us (29%)
  waiting for transfers between devices  81.9 us (24%)
  matrix products  53 us (16%)
  local copies, waits for them, and re-layouts  39.8 us (12%)
  starting transfers between devices  37.3 us (11%)
  other arithmetic  15.6 us (5%)
  between operations  13.8 us (4%)
    all_to_all x1, blocking collectives, local(): lax.all_to_all(own_keys, 'seq', split_axis=1, concat_axis=0, tiled=True)  67.3 us
    all_gather x1, waiting for transfers between devices, local(): lax.all_gather(local_values, 'blk', axis=0, tiled=True)  32.6 us
    all_to_all x1, blocking collectives, local(): lax.all_to_all(own_values, 'seq', split_axis=1, concat_axis=0, tiled=True)  29.7 us
    dot_general x8, matrix products, one_block(): jnp.einsum('hqk,khd->qhd', weights, value_block, preferred_element_type=j...  29 us
    dot_general x8, matrix products, one_block(): jnp.einsum('qhd,khd->hqk', grouped, key_block, preferred_element_type=jnp...  23.3 us
    all_to_all x1, waiting for transfers between devices, local(): lax.all_to_all(own_query, 'seq', split_axis=1, concat_axis=0, tiled=True)  23.1 us
    dynamic_slice x16, local copies, waits for them, and re-layouts, fold_keys(): state, unused = lax.scan(one_block, carry, (key_blocks, value_blocks))  16.8 us
    all_to_all x1, starting transfers between devices, sum_at_owner(): lax.all_to_all(split_up(array, dim, devices), axis, 0, 0, tiled=True)  13.1 us
  transfers between devices with their start and end apart: 10, of which 7 were waited for; matrix products, arithmetic and copies ran while one was open for 2% of the time, Pallas kernels for 0%

commit v1 on v0

--- a/solution.py
+++ b/solution.py
@@ -117,7 +117,10 @@
         start_for(frame_rows, heads),
         (
             lax.all_gather(local_keys, "blk", axis=0, tiled=True),
-            lax.all_gather(local_values, "blk", axis=0, tiled=True),
+            jnp.concatenate(
+                lax.all_to_all(jnp.stack([local_values] * lax.axis_size("blk")), "blk", 0, 0),
+                axis=0,
+            ),
         ),
         grouped,
         frame_rows,

time: 340 us -> 395 us (1.16)
  waiting for transfers between devices: 81.9 us -> 180 us
  blocking collectives: 97 us -> 0 us
  starting transfers between devices: 37.3 us -> 98.2 us
  local copies, waits for them, and re-layouts: 39.8 us -> 31 us
    all_to_all x2 -> x0, blocking collectives: 97 us -> none  [the longest x1 67.3 us: local(): lax.all_to_all(own_keys, 'seq', split_axis=1, concat_axis=0, tiled=True)]
    all_gather x1, waiting for transfers between devices: 0.02 us -> 78.4 us  [local(): lax.all_gather(local_keys, 'blk', axis=0, tiled=True)]
    all_to_all x0 -> x3, starting transfers between devices: none -> 57.5 us  [the longest x1 43.7 us: local(): lax.all_to_all(own_values, 'seq', split_axis=1, concat_axis=0, tiled=True)]
    all_to_all x0 -> x3, waiting for transfers between devices: none -> 52.3 us  [the longest x1 22.6 us: local(): lax.all_to_all(own_keys, 'seq', split_axis=1, concat_axis=0, tiled=True)]
    all_gather x1 -> x0, waiting for transfers between devices: 32.6 us -> none  [local(): lax.all_gather(local_values, 'blk', axis=0, tiled=True)]
    dynamic_slice x16 -> x8, local copies, waits for them, and re-layouts: 16.8 us -> 10.2 us  [fold_keys(): state, unused = lax.scan(one_block, carry, (key_blocks, value_blocks))]
    reshape x1 -> x0, local copies, waits for them, and re-layouts: 5.5 us -> none  [fold_keys(): value_blocks = values_piece.reshape(count, block, heads, HDIM)]
  transfers between devices with their start and end apart: 10 -> 12, of which waited for: 7 -> 10; matrix products, arithmetic and copies ran while one was open for 2% -> 3% of each run, Pallas kernels for 0% -> 0%
where the time goes in v1:
time: 395 us; the launch traced here: 394 us
  waiting for transfers between devices  180 us (46%)
  starting transfers between devices  98.2 us (25%)
  matrix products  54.8 us (14%)
  local copies, waits for them, and re-layouts  31 us (8%)
  other arithmetic  15.6 us (4%)
  between operations  13.8 us (3%)
    all_gather x1, waiting for transfers between devices, local(): lax.all_gather(local_keys, 'blk', axis=0, tiled=True)  78.4 us
    all_to_all x1, starting transfers between devices, local(): lax.all_to_all(own_values, 'seq', split_axis=1, concat_axis=0, tiled=True)  43.7 us
    dot_general x8, matrix products, one_block(): jnp.einsum('hqk,khd->qhd', weights, value_block, preferred_element_type=j...  30 us
    dot_general x8, matrix products, one_block(): jnp.einsum('qhd,khd->hqk', grouped, key_block, preferred_element_type=jnp...  24.2 us
    all_to_all x1, waiting for transfers between devices, local(): lax.all_to_all(own_keys, 'seq', split_axis=1, concat_axis=0, tiled=True)  22.6 us
    all_to_all x1, waiting for transfers between devices, local(): lax.all_to_all(own_query, 'seq', split_axis=1, concat_axis=0, tiled=True)  22.4 us
    all_to_all x1, waiting for transfers between devices, local(): lax.all_to_all(own_values, 'seq', split_axis=1, concat_axis=0, tiled=True)  21.8 us
    all_to_all x1, waiting for transfers between devices, sum_at_owner(): lax.all_to_all(split_up(array, dim, devices), axis, 0, 0, tiled=True)  13.3 us
  transfers between devices with their start and end apart: 12, of which 10 were waited for; matrix products, arithmetic and copies ran while one was open for 3% of the time, Pallas kernels for 0%

profile of v1, /device:TPU:66, one launch (start us, length us, event | category | flops | bytes accessed | tf_op | source)
XLA Modules:
  0.0 393.8 jit_solution(7235096622142404765)
XLA Ops:
  6.6 1.2 copy.72
  7.7 0.9 copy.52
  8.6 43.7 %all-to-all-start.2 = ((bf16[48,16,256]{2,0,1:T(8,128)(2,1)}), bf16[48,16,256]{2,0,1:T(8,128)(2,1)S(1)}, u32[]{:S(2)}, u32[]{:S(2)}) async-start(bf16[48,16,256]{2,0,1:T(8,128)(2,1)} %copy.52), calls=%async_computation.2 | async-start | bytes 786432 | tf_op jit(solution)/shard_map/all_to_all | solution.py:111
  52.3 1.1 copy.70
  53.3 0.9 copy.49
  54.2 21.8 %all-to-all-done.2 = bf16[48,16,256]{2,0,1:T(8,128)(2,1)S(1)} async-done(((bf16[48,16,256]{2,0,1:T(8,128)(2,1)}), bf16[48,16,256]{2,0,1:T(8,128)(2,1)S(1)}, u32[]{:S(2)}, u32[]{:S(2)}) %all-to-all-start.2) | async-done | bytes 393248 | tf_op jit(solution)/shard_map/all_to_all | solution.py:111
  76.0 6.1 %all-to-all-start = ((bf16[48,16,256]{2,0,1:T(8,128)(2,1)}), bf16[48,16,256]{2,0,1:T(8,128)(2,1)S(1)}, u32[]{:S(2)}, u32[]{:S(2)}) async-start(bf16[48,16,256]{2,0,1:T(8,128)(2,1)} %copy.49), calls=%async_computation | async-start | bytes 786432 | tf_op jit(solution)/shard_map/all_to_all | solution.py:110
  82.2 0.9 copy.51
  83.1 22.6 %all-to-all-done = bf16[48,16,256]{2,0,1:T(8,128)(2,1)S(1)} async-done(((bf16[48,16,256]{2,0,1:T(8,128)(2,1)}), bf16[48,16,256]{2,0,1:T(8,128)(2,1)S(1)}, u32[]{:S(2)}, u32[]{:S(2)}) %all-to-all-start) | async-done | bytes 393248 | tf_op jit(solution)/shard_map/all_to_all | solution.py:110
  105.7 6.2 %all-to-all-start.1 = ((bf16[48,16,256]{2,0,1:T(8,128)(2,1)}), bf16[48,16,256]{2,0,1:T(8,128)(2,1)S(1)}, u32[]{:S(2)}, u32[]{:S(2)}) async-start(bf16[48,16,256]{2,0,1:T(8,128)(2,1)} %copy.51), calls=%async_computation.1 | async-start | bytes 786432 | tf_op jit(solution)/shard_map/all_to_all | solution.py:109
  112.7 22.4 %all-to-all-done.1 = bf16[48,16,256]{2,0,1:T(8,128)(2,1)S(1)} async-done(((bf16[48,16,256]{2,0,1:T(8,128)(2,1)}), bf16[48,16,256]{2,0,1:T(8,128)(2,1)S(1)}, u32[]{:S(2)}, u32[]{:S(2)}) %all-to-all-start.1) | async-done | bytes 393248 | tf_op jit(solution)/shard_map/all_to_all | solution.py:109
  135.1 1.9 stack.5
  136.9 7.7 %all-to-all-start.3 = ((bf16[8,768,256]{1,2,0:T(8,128)(2,1)}), bf16[8,768,256]{1,2,0:T(8,128)(2,1)}, u32[]{:S(2)}, u32[]{:S(2)}) async-start(bf16[8,768,256]{1,2,0:T(8,128)(2,1)} %stack.5), calls=%async_computation.3 | async-start | bytes 6291456 | tf_op jit(solution)/shard_map/all_to_all | solution.py:121
  144.8 78.4 %all-gather.2.cloned.1.call-done = bf16[6144,256]{1,0:T(8,128)(2,1)} async-done(((bf16[768,256]{1,0:T(8,128)(2,1)}), bf16[6144,256]{1,0:T(8,128)(2,1)}) %all-gather.2.cloned.1.call-update) | async-done | bytes 3145744 | tf_op jit(solution)/shard_map/all_gather | solution.py:119
  223.2 5.5 %reshape.64 = bf16[8,768,2,128]{3,2,1,0:T(2,128)(2,1)} reshape(bf16[6144,256]{1,0:T(8,128)(2,1)} %all-gather.2.cloned.1.call-done) | data formatting | bytes 6291456 | tf_op jit(solution)/shard_map/reshape | solution.py:47
  228.7 7.9 %all-to-all-done.3 = bf16[8,768,256]{1,2,0:T(8,128)(2,1)} async-done(((bf16[8,768,256]{1,2,0:T(8,128)(2,1)}), bf16[8,768,256]{1,2,0:T(8,128)(2,1)}, u32[]{:S(2)}, u32[]{:S(2)}) %all-to-all-start.3) | async-done | bytes 3145760 | tf_op jit(solution)/shard_map/all_to_all | solution.py:121
  236.6 72.0 %while.15 = (s32[]{:T(128)}, f32[2,768]{1,0:T(2,128)S(1)}, f32[2,768]{1,0:T(2,128)S(1)}, f32[768,2,128]{0,2,1:T(8,128)S(1)}, bf16[8,768,2,128]{3,2,1,0:T(2,128)(...) while((s32[]{:T(128)}, f32[2,768]{1,0:T(2,128)S(1)}, ...), condition=%wide.region_3.4_spmd.clone, body=%wide.region_0.3_spmd.clone.sunk | while | flops 614016000 | bytes 36668040 | solution.py:69
  236.6 1.3 constant_dynamic-slice_fusion.2
  237.9 3.0 bitcast_reduce_fusion.2
  241.0 3.8 fusion.56
  244.8 0.8 fusion.54
  245.7 1.3 constant_dynamic-slice_fusion.2
  246.9 3.0 bitcast_reduce_fusion.2
  250.0 3.7 fusion.56
  253.8 0.8 fusion.54
  254.7 1.3 constant_dynamic-slice_fusion.2
  255.9 3.0 bitcast_reduce_fusion.2
  259.0 3.8 fusion.56
  262.8 0.8 fusion.54
  263.7 1.3 constant_dynamic-slice_fusion.2
  264.9 3.0 bitcast_reduce_fusion.2
  268.0 3.8 fusion.56
  271.8 0.8 fusion.54
  272.7 1.3 constant_dynamic-slice_fusion.2
  273.9 3.0 bitcast_reduce_fusion.2
  277.0 3.7 fusion.56
  280.8 0.8 fusion.54
  281.6 1.3 constant_dynamic-slice_fusion.2
  282.9 3.0 bitcast_reduce_fusion.2
  286.0 3.8 fusion.56
  289.8 0.8 fusion.54
  290.6 1.3 constant_dynamic-slice_fusion.2
  291.9 3.0 bitcast_reduce_fusion.2
  295.0 3.8 fusion.56
  299.6 1.3 constant_dynamic-slice_fusion.2
  300.9 3.0 bitcast_reduce_fusion.2
  304.0 3.7 fusion.56
  307.8 0.8 fusion.54
  309.1 0.8 reshape.65
  309.9 13.1 %all-to-all-start.4 = ((bf16[16,2,1536]{2,1,0:T(2,128)(2,1)}), bf16[16,2,1536]{2,1,0:T(2,128)(2,1)S(1)}, u32[]{:S(2)}, u32[]{:S(2)}) async-start(bf16[16,2,1536]{2,1,0:T(2,128)(2,1)} %reshape.65), calls=%async_computation.4 | async-start | bytes 196608 | tf_op jit(solution)/shard_map/all_to_all | solution.py:22
  323.0 13.3 %all-to-all-done.4 = bf16[16,2,1536]{2,1,0:T(2,128)(2,1)S(1)} async-done(((bf16[16,2,1536]{2,1,0:T(2,128)(2,1)}), bf16[16,2,1536]{2,1,0:T(2,128)(2,1)S(1)}, u32[]{:S(2)}, u32[]{:S(2)}) %all-to-all-start.4) | async-done | bytes 98336 | tf_op jit(solution)/shard_map/all_to_all | solution.py:22
  336.6 2.1 collective-permute-start
  341.2 8.8 %reduce = bf16[1536,2]{1,0:T(8,128)(2,1)S(1)} reduce(bf16[1536,1,2]{2,1,0:T(2,128)(2,1)S(1)} %bitcast.78, bf16[]{:T(256)} %broadcast.59), dimensions={1}, to_apply=%bitcast.54.reduce_sub_computation | reduce | bytes 12290
  350.0 1.1 reshape.67
  351.1 8.8 %all-to-all-start.5 = ((bf16[8,2,192]{2,1,0:T(2,128)(2,1)}), bf16[8,2,192]{2,1,0:T(2,128)(2,1)S(1)}, u32[]{:S(2)}, u32[]{:S(2)}) async-start(bf16[8,2,192]{2,1,0:T(2,128)(2,1)} %reshape.67), calls=%async_computation.5 | async-start | bytes 16384 | tf_op jit(solution)/shard_map/all_to_all | solution.py:155
  360.0 6.3 %all-to-all-done.5 = bf16[8,2,192]{2,1,0:T(2,128)(2,1)S(1)} async-done(((bf16[8,2,192]{2,1,0:T(2,128)(2,1)}), bf16[8,2,192]{2,1,0:T(2,128)(2,1)S(1)}, u32[]{:S(2)}, u32[]{:S(2)}) %all-to-all-start.5) | async-done | bytes 6176 | tf_op jit(solution)/shard_map/all_to_all | solution.py:155
  366.3 0.9 reshape.68
  367.9 3.1 collective-permute-start.1
  371.1 1.3 collective-permute-start.2
  372.5 4.1 %collective-permute-done.2 = bf16[6,1,6,16]{3,0,2,1:T(8,128)(2,1)S(1)} collective-permute-done((bf16[6,1,6,16]{3,0,2,1:T(8,128)(2,1)S(1)}, bf16[6,1,6,16]{3,0,2,1:T(8,128)(2,1)S(1)}, u32[]{:S(2)}, u32[]{:S(2)}) %collective-permute-start.2) | collective-permute-done | bytes 1184 | tf_op jit(solution)/shard_map/ppermute | solution.py:38
  376.7 2.5 collective-permute-start.3
  379.2 3.4 collective-permute-start.4
  382.7 2.1 collective-permute-done.4
  385.0 1.0 concatenate.48
  (103 shorter events, 8.0 us)
Async XLA Ops:
  6.5 302.2 %copy-start = (bf16[4096,64]{0,1:T(8,128)(2,1)S(1)}, bf16[4096,64]{0,1:T(8,128)(2,1)}, u32[]{:S(2)}) copy-start(bf16[4096,64]{0,1:T(8,128)(2,1)} %param.17) | copy-start | bytes 1572868
  6.6 75.6 %copy-start.3 = (bf16[1,48,4096]{2,1,0:T(8,128)(2,1)S(1)}, bf16[1,48,4096]{2,1,0:T(8,128)(2,1)}, u32[]{:S(2)}) copy-start(bf16[1,48,4096]{2,1,0:T(8,128)(2,1)} %param.12) | copy-start | bytes 1179652
  8.6 67.4 %all-to-all-start.2 = ((bf16[48,16,256]{2,0,1:T(8,128)(2,1)}), bf16[48,16,256]{2,0,1:T(8,128)(2,1)S(1)}, u32[]{:S(2)}, u32[]{:S(2)}) async-start(bf16[48,16,256]{2,0,1:T(8,128)(2,1)} %copy.52), calls=%async_computation.2 | async-start | bytes 786432 | tf_op jit(solution)/shard_map/all_to_all | solution.py:111
  76.0 29.8 %all-to-all-start = ((bf16[48,16,256]{2,0,1:T(8,128)(2,1)}), bf16[48,16,256]{2,0,1:T(8,128)(2,1)S(1)}, u32[]{:S(2)}, u32[]{:S(2)}) async-start(bf16[48,16,256]{2,0,1:T(8,128)(2,1)} %copy.49), calls=%async_computation | async-start | bytes 786432 | tf_op jit(solution)/shard_map/all_to_all | solution.py:110
  105.7 6.4 %copy-start.2 = (bf16[48,16,256]{2,0,1:T(8,128)(2,1)}, bf16[48,16,256]{2,0,1:T(8,128)(2,1)S(1)}, u32[]{:S(2)}) copy-start(bf16[48,16,256]{2,0,1:T(8,128)(2,1)S(1)} %all-to-all-done) | copy-start | bytes 1179652
  105.7 29.3 %all-to-all-start.1 = ((bf16[48,16,256]{2,0,1:T(8,128)(2,1)}), bf16[48,16,256]{2,0,1:T(8,128)(2,1)S(1)}, u32[]{:S(2)}, u32[]{:S(2)}) async-start(bf16[48,16,256]{2,0,1:T(8,128)(2,1)} %copy.51), calls=%async_computation.1 | async-start | bytes 786432 | tf_op jit(solution)/shard_map/all_to_all | solution.py:109
  111.9 111.3 %all-gather.2.cloned.1.call-start = ((), (), s32[]{:S(2)}) async-start(), calls=%async_computation.6 | async-start | bytes 3538944 | tf_op jit(solution)/shard_map/all_gather | solution.py:119
  136.9 99.7 %all-to-all-start.3 = ((bf16[8,768,256]{1,2,0:T(8,128)(2,1)}), bf16[8,768,256]{1,2,0:T(8,128)(2,1)}, u32[]{:S(2)}, u32[]{:S(2)}) async-start(bf16[8,768,256]{1,2,0:T(8,128)(2,1)} %stack.5), calls=%async_computation.3 | async-start | bytes 6291456 | tf_op jit(solution)/shard_map/all_to_all | solution.py:121
  236.6 102.1 %copy-start.9 = (s32[48]{0:T(128)S(1)}, s32[48]{0:T(128)}, u32[]{:S(2)}) copy-start(s32[48]{0:T(128)} %param.16) | copy-start | bytes 580
  236.6 102.2 %copy-start.5 = (f32[48,64]{1,0:T(8,128)S(1)}, f32[48,64]{1,0:T(8,128)}, u32[]{:S(2)}) copy-start(f32[48,64]{1,0:T(8,128)} %param.15) | copy-start | bytes 36868
  236.6 102.2 %copy-start.7 = (f32[16]{0:T(128)S(1)}, f32[16]{0:T(128)}, u32[]{:S(2)}) copy-start(f32[16]{0:T(128)} %param.19) | copy-start | bytes 196
  236.6 102.3 %copy-start.8 = (f32[16]{0:T(128)S(1)}, f32[16]{0:T(128)}, u32[]{:S(2)}) copy-start(f32[16]{0:T(128)} %param.18) | copy-start | bytes 196
  241.0 3.9 copy-start.1
  250.0 3.9 copy-start.1
  259.0 3.9 copy-start.1
  268.0 3.9 copy-start.1
  277.0 3.9 copy-start.1
  285.9 3.9 copy-start.1
  294.9 3.9 copy-start.1
  303.9 3.9 copy-start.1
  308.7 77.4 %copy-start.4 = (bf16[3,3,3,16,384]{4,3,2,1,0:T(8,128)(2,1)S(1)}, bf16[3,3,3,16,384]{4,3,2,1,0:T(8,128)(2,1)}, u32[]{:S(2)}) copy-start(bf16[3,3,3,16,384]{4,3,2,1,0:T(8,128)(2,1)} %param.20) | copy-start | bytes 995332
  308.7 77.4 %copy-start.6 = (f32[384]{0:T(512)S(1)}, f32[384]{0:T(512)}, u32[]{:S(2)}) copy-start(f32[384]{0:T(512)} %param.21) | copy-start | bytes 4612
  309.9 26.4 %all-to-all-start.4 = ((bf16[16,2,1536]{2,1,0:T(2,128)(2,1)}), bf16[16,2,1536]{2,1,0:T(2,128)(2,1)S(1)}, u32[]{:S(2)}, u32[]{:S(2)}) async-start(bf16[16,2,1536]{2,1,0:T(2,128)(2,1)} %reshape.65), calls=%async_computation.4 | async-start | bytes 196608 | tf_op jit(solution)/shard_map/all_to_all | solution.py:22
  336.6 3.1 collective-permute-start
  351.1 15.1 %all-to-all-start.5 = ((bf16[8,2,192]{2,1,0:T(2,128)(2,1)}), bf16[8,2,192]{2,1,0:T(2,128)(2,1)S(1)}, u32[]{:S(2)}, u32[]{:S(2)}) async-start(bf16[8,2,192]{2,1,0:T(2,128)(2,1)} %reshape.67), calls=%async_computation.5 | async-start | bytes 16384 | tf_op jit(solution)/shard_map/all_to_all | solution.py:155
  367.9 4.6 %collective-permute-start.1 = (bf16[6,1,6,16]{3,0,2,1:T(8,128)(2,1)S(1)}, bf16[6,1,6,16]{3,0,2,1:T(8,128)(2,1)S(1)}, u32[]{:S(2)}, u32[]{:S(2)}) collective-permute-start(bf16[6,1,6,16]{3,0,2,1:T(8,128)(2,1)S(1)} %get-tuple-element.149), channel_id=1, source_target_pairs={{0,16},{16,32},{32,48},{48,64},{64,80},{80,96},{96,112},{112,128},... | collective-permute-start | bytes 3464 | tf_op jit(solution)/shard_map/ppermute | solution.py:37
  371.1 5.6 %collective-permute-start.2 = (bf16[6,1,6,16]{3,0,2,1:T(8,128)(2,1)S(1)}, bf16[6,1,6,16]{3,0,2,1:T(8,128)(2,1)S(1)}, u32[]{:S(2)}, u32[]{:S(2)}) collective-permute-start(bf16[6,1,6,16]{3,0,2,1:T(8,128)(2,1)S(1)} %get-tuple-element.150), channel_id=1, source_target_pairs={{16,0},{32,16},{48,32},{64,48},{80,64},{96,80},{112,96},{128,112},... | collective-permute-start | bytes 3464 | tf_op jit(solution)/shard_map/ppermute | solution.py:38
  376.7 6.0 %collective-permute-start.3 = (bf16[6,6,1,16]{3,0,2,1:T(8,128)(2,1)S(1)}, bf16[6,6,1,16]{3,0,2,1:T(8,128)(2,1)S(1)}, u32[]{:S(2)}, u32[]{:S(2)}) collective-permute-start(bf16[6,6,1,16]{3,0,2,1:T(8,128)(2,1)S(1)} %get-tuple-element.136), channel_id=1, source_target_pairs={{0,2},{2,4},{4,6},{6,8},{8,10},{10,12},{12,14},{1,3},{3,5},{5,7},{... | collective-permute-start | bytes 3464 | tf_op jit(solution)/shard_map/ppermute | solution.py:37
  379.2 5.6 %collective-permute-start.4 = (bf16[6,6,1,16]{3,0,2,1:T(8,128)(2,1)S(1)}, bf16[6,6,1,16]{3,0,2,1:T(8,128)(2,1)S(1)}, u32[]{:S(2)}, u32[]{:S(2)}) collective-permute-start(bf16[6,6,1,16]{3,0,2,1:T(8,128)(2,1)S(1)} %get-tuple-element.135), channel_id=1, source_target_pairs={{2,0},{4,2},{6,4},{8,6},{10,8},{12,10},{14,12},{3,1},{5,3},{7,5},{... | collective-permute-start | bytes 3464 | tf_op jit(solution)/shard_map/ppermute | solution.py:38
Sparse Core Ops, SparseCore 0:
  114.9 108.3 all-gather.1
